TPU v7x, 32 devices: a whole 2x2x4 slice. The times are simulated.
32 devices in a mesh: side: 8 (over y, x, core), lane: 4 (over z).
Axes of the slice: x: 2, y: 2, z: 4, core: 2. Of those that a mesh axis runs over, the one named last changes fastest.
Arguments:
- tokens: bfloat16 [4096, 2048], P(('side', 'lane')), may hold values from -6 to 6
- expert_ids: int32 [4096, 8], P(('side', 'lane')), may hold values from 0 to 31, all different within a row; in each aligned block of 128 rows (0 to 127, 128 to 255, ...) at most 64 rows name the same one
- route_weights: float32 [4096, 8], P(('side', 'lane')), may hold values from 0.03 to 0.4
- w_gate: bfloat16 [32, 2048, 768], P(('side', 'lane')), may hold values from -0.125 to 0.125
- w_up: bfloat16 [32, 2048, 768], P(('side', 'lane')), may hold values from -0.125 to 0.125
- w_down: bfloat16 [32, 768, 2048], P(('side', 'lane')), may hold values from -0.21875 to 0.21875
Outputs:
- mixed: bfloat16 [4096, 2048], P(('side', 'lane'))
Inputs may be any that keep to these rules, and one draw needn't show every extreme that they name: `expert_ids`: each row names 8 different experts. Within each aligned block of 128 rows (the rows of one device) no expert is named by more than 64 rows, and in every draw some expert is named by exactly 64 rows of some block.
All inputs are finite; a program needn't handle non-finite values.
Results may differ from a plain program's by a relative error of at most 0.0085.
Values may be sent and summed in bfloat16 or wider, within the bound.
A program may use at most 128 MiB of HBM per device.

v0:
```python
import functools

import jax
import jax.numpy as jnp
from jax import lax
from jax.experimental import pallas as pl
from jax.experimental.pallas import tpu as pltpu
from jax.sharding import PartitionSpec as P

AXES = ("side", "lane")
MESH = pl.DeviceIdType.MESH
BF16 = jnp.bfloat16
F32 = jnp.float32


def flip(value, mask):
    bit = 1
    out = value
    while bit <= mask:
        if mask & bit:
            out = out + bit - 2 * bit * ((value // bit) % 2)
        bit *= 2
    return out


def place(levels):
    side = lax.axis_index("side")
    level = lax.axis_index("lane")
    return side // 2, side % 2, level


def greet(devices):
    barrier = pltpu.get_barrier_semaphore()
    for device in devices:
        pl.semaphore_signal(barrier, inc=1, device_id=device, device_id_type=MESH)
    pl.semaphore_wait(barrier, len(devices))


def gather_kernel(
    levels, tokens, mine, wg, wu, wd, every, shares, wg2, wu2, wd2, send, recv, ssend, srecv, wsend, wrecv, local
):
    col, core, level = place(levels)
    half = tokens.shape[0] // 2
    chips = every.shape[0]
    col_x, col_y = flip(col, 1), flip(col, 2)
    dev_x, dev_y = (col_x * 2 + core, level), (col_y * 2 + core, level)
    twin = (col * 2 + 1 - core, level)
    me = col * levels + level
    others = [
        (flip(col, m // levels), flip(level, m % levels)) for m in range(1, chips)
    ]
    greet([(q * 2 + core, z) for q, z in others] + [twin])

    started = []

    def go(src, dst, s, r, device):
        copy = pltpu.make_async_remote_copy(
            src_ref=src, dst_ref=dst, send_sem=s, recv_sem=r, device_id=device, device_id_type=MESH
        )
        copy.start()
        started.append(copy)
        return copy

    for i, (q, z) in enumerate(others):
        go(mine.at[q * levels + z], shares.at[me], ssend.at[i], srecv.at[i], (q * 2 + core, z))
    keep = [
        pltpu.make_async_copy(tokens, every.at[me], local.at[0]),
        pltpu.make_async_copy(mine.at[me], shares.at[me], local.at[1]),
    ]
    for copy in keep:
        copy.start()

    lanes = []
    top, low = pl.ds(0, half), pl.ds(half, half)
    waited = set()
    for k in range(levels):
        z = flip(level, k)
        b = col * levels + z
        if k:
            lanes[k - 1].wait_recv()
            waited.add(id(lanes[k - 1]))
            block = every.at[b]
        else:
            block = tokens
        a = go(block.at[top], every.at[b, top], send.at[1, k], recv.at[1, k], dev_x)
        c = go(block.at[low], every.at[b, low], send.at[2, k], recv.at[2, k], dev_y)
        if k == 0:
            for m in range(1, levels):
                lanes.append(
                    go(tokens, every.at[me], send.at[0, m], recv.at[0, m], (col * 2 + core, flip(level, m)))
                )
        go(block.at[low], every.at[b, low], send.at[3, k], recv.at[3, k], dev_x)
        go(block.at[top], every.at[b, top], send.at[4, k], recv.at[4, k], dev_y)
        if k == 0:
            go(wg, wg2, wsend.at[0], wrecv.at[0], twin)
            go(wu, wu2, wsend.at[1], wrecv.at[1], twin)
            go(wd, wd2, wsend.at[2], wrecv.at[2], twin)
        a.wait_recv()
        waited.add(id(a))
        bx = every.at[col_x * levels + z, top]
        go(bx, bx, send.at[5, k], recv.at[5, k], dev_y)
        c.wait_recv()
        waited.add(id(c))
        by = every.at[col_y * levels + z, low]
        go(by, by, send.at[6, k], recv.at[6, k], dev_x)
    for copy in started:
        if id(copy) not in waited:
            copy.wait_recv()
        copy.wait_send()
    for copy in keep:
        copy.wait()


def return_kernel(
    levels, every, pick, back, wga, wua, wda, wgb, wub, wdb, out, wgs, wus, wds, xs, ys, part, first,
    second, third, fold, level_sum, send, recv, fetch
):
    loads = [
        pltpu.make_async_copy(src.at[0], dst.at[e], fetch.at[i, e])
        for i, (dst, pair) in enumerate(((wgs, (wga, wgb)), (wus, (wua, wub)), (wds, (wda, wdb))))
        for e, src in enumerate(pair)
    ]
    for copy in loads:
        copy.start()
    col, core, level = place(levels)
    rows = out.shape[0]
    half = rows // 2
    col_x, col_y, col_xy = flip(col, 1), flip(col, 2), flip(flip(col, 1), 2)
    dev_x, dev_y = (col_x * 2 + core, level), (col_y * 2 + core, level)
    greet([dev_x, dev_y] + [(col * 2 + core, flip(level, m)) for m in range(1, levels)])
    top, low = pl.ds(0, half), pl.ds(half, half)
    started = []

    def go(src, dst, i, k, device):
        copy = pltpu.make_async_remote_copy(
            src_ref=src,
            dst_ref=dst,
            send_sem=send.at[i, k],
            recv_sem=recv.at[i, k],
            device_id=device,
            device_id_type=MESH,
        )
        copy.start()
        started.append(copy)
        return copy

    def add(dst, one, two):
        dst[...] = (one[...].astype(F32) + two[...].astype(F32)).astype(BF16)

    columns = every.shape[0] // levels
    slots = pick.shape[1] // 2

    def compute(k):
        z = flip(level, k)
        for j in range(columns):
            b = j * levels + z
            rows_b = jnp.dot(pick[b], every[b], preferred_element_type=F32).astype(BF16)
            for e in range(2):
                xs[e, pl.ds(j * slots, slots)] = rows_b[e * slots : (e + 1) * slots]

        def expert(e, carry):
            x = xs[e]
            gate = jnp.dot(x, wgs[e], preferred_element_type=F32)
            upper = jnp.dot(x, wus[e], preferred_element_type=F32)
            hidden = (gate / (1.0 + jnp.exp(-gate)) * upper).astype(BF16)
            ys[e] = jnp.dot(hidden, wds[e], preferred_element_type=F32).astype(BF16)
            return carry

        lax.fori_loop(0, 2, expert, 0)
        for j in range(columns):
            b = j * levels + z
            mix = back[b]
            y = jnp.concatenate([ys[e, pl.ds(j * slots, slots)] for e in range(2)], axis=0)
            part[b] = jnp.dot(mix, y, preferred_element_type=F32).astype(BF16)

    def stage_one(k):
        z = flip(level, k)
        return [
            go(part.at[col_xy * levels + z, top], first.at[k, 0, 0], 0, k, dev_x),
            go(part.at[col_xy * levels + z, low], first.at[k, 1, 0], 1, k, dev_y),
            go(part.at[col_x * levels + z, top], first.at[k, 0, 1], 2, k, dev_x),
            go(part.at[col_y * levels + z, low], first.at[k, 1, 1], 3, k, dev_y),
        ]

    def stage_two(k, ones):
        z = flip(level, k)
        ones[0].wait_recv()
        add(fold.at[k, 0], part.at[col_y * levels + z, top], first.at[k, 0, 0])
        a = go(fold.at[k, 0], second.at[k, 0], 4, k, dev_y)
        ones[1].wait_recv()
        add(fold.at[k, 1], part.at[col_x * levels + z, low], first.at[k, 1, 0])
        b = go(fold.at[k, 1], second.at[k, 1], 5, k, dev_x)
        return [a, b]

    def stage_three(k, ones, twos):
        z = flip(level, k)
        for copy in ones[2:] + twos:
            copy.wait_recv()
        for h, piece in enumerate((top, low)):
            level_sum[k, piece] = (
                part[col * levels + z, piece].astype(F32)
                + first[k, h, 1].astype(F32)
                + second[k, h].astype(F32)
            ).astype(BF16)
        if k:
            return go(level_sum.at[k], third.at[k], 6, k, (col * 2 + core, flip(level, k)))

    order = list(range(levels - 1, -1, -1))
    ones, twos, threes = {}, {}, {}
    for copy in loads:
        copy.wait()
    for n in range(levels + 2):
        if n < levels:
            compute(order[n])
            ones[order[n]] = stage_one(order[n])
        if 1 <= n <= levels:
            p = order[n - 1]
            twos[p] = stage_two(p, ones[p])
        if n >= 2:
            p = order[n - 2]
            threes[p] = stage_three(p, ones[p], twos[p])
    for m in range(1, levels):
        threes[m].wait_recv()
    total = level_sum[0].astype(F32)
    for m in range(1, levels):
        total = total + third[m].astype(F32)
    out[...] = total.astype(BF16)
    for copy in started:
        copy.wait_send()


def on_layers(levels, tokens, expert_ids, route_weights, w_gate, w_up, w_down):
    tok_rows, width = tokens.shape
    top_count = expert_ids.shape[1]
    device_count = lax.axis_size("side") * levels
    capacity = 2 * tok_rows * top_count // device_count
    chips = device_count // 2
    core = lax.axis_index("side") % 2
    experts = jnp.arange(device_count, dtype=jnp.int32)
    weight = jnp.sum(
        jnp.where(expert_ids[:, None, :] == experts[None, :, None], route_weights[:, None, :], 0.0),
        axis=2,
    ).T
    mine = weight.reshape(chips // levels, 2, levels, tok_rows).transpose(0, 2, 1, 3)
    mine = mine.reshape(chips, 2, tok_rows)
    mine = jnp.where(core == 1, mine[:, ::-1], mine)
    mine = jnp.pad(mine, ((0, 0), (0, 6), (0, 0)))
    anywhere = pl.BlockSpec(memory_space=pl.ANY)
    dma = pltpu.SemaphoreType.DMA
    shape = jax.ShapeDtypeStruct
    every, shares, wg2, wu2, wd2 = pl.pallas_call(
        functools.partial(gather_kernel, levels),
        out_shape=[
            shape((chips, tok_rows, width), BF16),
            shape(mine.shape, F32),
            shape(w_gate.shape, BF16),
            shape(w_up.shape, BF16),
            shape(w_down.shape, BF16),
        ],
        in_specs=[anywhere] * 5,
        out_specs=[anywhere] * 5,
        scratch_shapes=[
            dma((7, levels)),
            dma((7, levels)),
            dma((chips - 1,)),
            dma((chips - 1,)),
            dma((3,)),
            dma((3,)),
            dma((2,)),
        ],
        compiler_params=pltpu.CompilerParams(collective_id=0, has_side_effects=True),
        name="spread",
    )(tokens, mine, w_gate, w_up, w_down)

    weights = shares[:, :2]
    chosen = weights > 0.0
    before = jnp.triu(jnp.ones((tok_rows, tok_rows), BF16), 1)
    slot = jnp.dot(chosen.astype(BF16).reshape(chips * 2, tok_rows), before, preferred_element_type=F32)
    slot = slot.reshape(chips, 2, tok_rows).astype(jnp.int32)
    table = (
        slot[:, :, None, :] == jnp.arange(capacity, dtype=jnp.int32)[None, None, :, None]
    ) & chosen[:, :, None, :]
    pick = table.astype(BF16)
    back = jnp.where(table, weights[:, :, None, :], 0.0).astype(BF16)
    back = back.reshape(chips, 2 * capacity, tok_rows).transpose(0, 2, 1)
    pick = pick.reshape(chips, 2 * capacity, tok_rows)
    half = tok_rows // 2
    vmem = pl.BlockSpec(memory_space=pltpu.VMEM)
    return pl.pallas_call(
        functools.partial(return_kernel, levels),
        out_shape=shape((tok_rows, width), BF16),
        in_specs=[vmem] * 3 + [anywhere] * 6,
        out_specs=vmem,
        scratch_shapes=[
            pltpu.VMEM((2,) + w_gate.shape[1:], BF16),
            pltpu.VMEM((2,) + w_up.shape[1:], BF16),
            pltpu.VMEM((2,) + w_down.shape[1:], BF16),
            pltpu.VMEM((2, chips // levels * capacity, width), BF16),
            pltpu.VMEM((2, chips // levels * capacity, width), BF16),
            pltpu.VMEM((chips, tok_rows, width), BF16),
            pltpu.VMEM((levels, 2, 2, half, width), BF16),
            pltpu.VMEM((levels, 2, half, width), BF16),
            pltpu.VMEM((levels, tok_rows, width), BF16),
            pltpu.VMEM((levels, 2, half, width), BF16),
            pltpu.VMEM((levels, tok_rows, width), BF16),
            dma((7, levels)),
            dma((7, levels)),
            dma((3, 2)),
        ],
        compiler_params=pltpu.CompilerParams(
            collective_id=1, has_side_effects=True, vmem_limit_bytes=60 * 2**20
        ),
        name="collect",
    )(every, pick, back, w_gate, w_up, w_down, wg2, wu2, wd2)


def expert_ffn(rows, gate_proj, up_proj, down_proj):
    gate = jnp.dot(rows, gate_proj, preferred_element_type=jnp.float32)
    upper = jnp.dot(rows, up_proj, preferred_element_type=jnp.float32)
    hidden = (jax.nn.silu(gate) * upper).astype(jnp.bfloat16)
    return jnp.dot(hidden, down_proj, preferred_element_type=jnp.float32).astype(jnp.bfloat16)


def on_device(tokens, expert_ids, route_weights, w_gate, w_up, w_down):
    tok_rows = tokens.shape[0]
    width = tokens.shape[1]
    top_count = expert_ids.shape[1]
    side_count = lax.axis_size("side")
    device_count = side_count * lax.axis_size("lane")
    local_count = w_gate.shape[0]
    expert_count = device_count * local_count
    capacity = 2 * tok_rows * top_count // expert_count
    flat_ids = expert_ids.reshape(-1)
    onehot = (flat_ids[:, None] == jnp.arange(expert_count, dtype=jnp.int32)[None, :]).astype(
        jnp.int32
    )
    earlier = jnp.cumsum(onehot, axis=0) - onehot
    slot_index = jnp.sum(earlier * onehot, axis=1)
    position = (flat_ids * capacity + slot_index).reshape(tok_rows, top_count)
    buffer_rows = jnp.arange(expert_count * capacity, dtype=jnp.int32)
    dispatch_table = jnp.any(buffer_rows[:, None, None] == position[None, :, :], axis=2).astype(
        jnp.bfloat16
    )
    outgoing = jnp.dot(dispatch_table, tokens, preferred_element_type=jnp.float32).astype(
        jnp.bfloat16
    )
    outgoing = outgoing.reshape(expert_count, capacity, width)
    received = lax.all_to_all(outgoing, ("side", "lane"), split_axis=0, concat_axis=0, tiled=True)
    count = received.shape[1]
    grouped = received.reshape(device_count, local_count, count, width)
    rows = grouped[:, 0].reshape(device_count * count, width)
    output = expert_ffn(rows, w_gate[0], w_up[0], w_down[0])
    results = [output.reshape(device_count, count, width)]
    returned = lax.all_to_all(
        jnp.stack(results, axis=1).reshape(device_count * local_count, count, width),
        ("side", "lane"),
        split_axis=0,
        concat_axis=0,
        tiled=True,
    )
    flat_back = returned.reshape(expert_count * capacity, width)
    picked = flat_back[position]
    mixed = jnp.einsum("tk,tkd->td", route_weights, picked, preferred_element_type=jnp.float32)
    return mixed.astype(jnp.bfloat16)


def layered(mesh, tokens):
    side, levels = mesh.shape["side"], mesh.shape["lane"]
    layer_bytes = tokens.shape[0] // 2 * tokens.shape[1] * tokens.dtype.itemsize
    return side == 2**3 and levels & (levels - 1) == 0 and 3 * layer_bytes < 32 * 2**20


def solution(mesh):
    placed = (
        P(AXES, None),
        P(AXES, None),
        P(AXES, None),
        P(AXES, None, None),
        P(AXES, None, None),
        P(AXES, None, None),
    )

    def run(tokens, *rest):
        body = on_device
        if layered(mesh, tokens):
            body = functools.partial(on_layers, mesh.shape["lane"])
        return jax.shard_map(
            body, mesh=mesh, in_specs=placed, out_specs=P(AXES, None), check_vma=False
        )(tokens, *rest)

    return run
```

profile of v0, /device:TPU:0, one launch (start us, length us, event | category | flops | bytes accessed | tf_op | source)
XLA Modules:
  0.0 189.8 jit_solution(15552887209450626975)
XLA Ops:
  0.0 0.7 select_reduce_fusion
  0.8 0.6 pad.4.mine
  1.5 84.3 %spread.1 = (bf16[16,128,2048]{2,1,0:T(8,128)(2,1)}, f32[16,8,128]{2,1,0:T(8,128)}, bf16[1,2048,768]{2,1,0:T(8,128)(2,1)}, bf16[1,2048,768]{2,1,0:T(8,128)(2,1)}, bf16[1,768,2048]{2,1,0:T(8,128)(2,1)}) custom-call(bf16[128,2048]{1,0:T(8,128)(2,1)} %tokens.1, f32[16,8,128]{2,1,0:T(8,128)} %pad.4.mine, bf16[1,2048,768]{2,1,0:T(8,128)(2,1)} %wga.1, ...), custom_call_target="tpu_custom_call" | custom-call | tf_op jit(solution)/shard_map/spread/pallas_call | solution.py:251
  85.8 0.9 broadcast_compare_fusion
  86.7 0.1 convolution_convert_fusion
  86.8 0.1 eq.43
  86.9 0.3 copy.26
  87.2 0.8 slice.3
  88.1 0.1 broadcast_in_dim.44
  88.1 0.3 copy.28
  88.4 0.1 and.19
  88.5 0.4 copy.27
  89.0 0.1 eq.46
  89.1 1.1 fusion
  90.2 0.1 convert_element_type.15
  90.3 1.0 copy.29.pick
  91.4 96.5 %collect.1 = bf16[128,2048]{1,0:T(8,128)(2,1)} custom-call(bf16[16,128,2048]{2,1,0:T(8,128)(2,1)} %get-tuple-element.10.every, bf16[16,128,128]{2,1,0:T(8,128)(2,1)} %copy.29.pick, bf16[16,128,128]{2,1,0:T(8,128)(2,1)} %get-tuple-element.15.back, bf16[1,2048,768]{2,1,0:T(8,128)(2,1)} %wga.1, bf16[1,2048,768]{2,1,0:T(8,128)(2,1)} %wua.1, ...), custom_call_target="tpu_custom_call" | custom-call | tf_op jit(solution)/shard_map/collect/pallas_call | solution.py:289
  187.9 1.9 copy.33
  (5 shorter events, 0.1 us)
where the time goes:
time: 190 us
  Pallas kernels  181 us (95%)
  local copies, waits for them, and re-layouts  5.82 us (3%)
  other arithmetic  2.89 us (2%)
    pallas_call x1, Pallas kernels, on_layers(): pl.pallas_call(functools.partial(return_kernel, levels), out_shape=shape(...  96.5 us
    pallas_call x1, Pallas kernels, on_layers(): pl.pallas_call(functools.partial(gather_kernel, levels), out_shape=[shape...  84.3 us

commit v1 on v0

v1 whole, which is shorter than its diff:
```python
import functools

import jax
import jax.numpy as jnp
from jax import lax
from jax.experimental import pallas as pl
from jax.experimental.pallas import tpu as pltpu
from jax.sharding import PartitionSpec as P

AXES = ("side", "lane")
MESH = pl.DeviceIdType.MESH
BF16 = jnp.bfloat16
F32 = jnp.float32


def flip(value, mask):
    bit = 1
    out = value
    while bit <= mask:
        if mask & bit:
            out = out + bit - 2 * bit * ((value // bit) % 2)
        bit *= 2
    return out


def fused_kernel(
    levels, spare, tokens, ids, gains, wg, wu, wd, out, ids_v, gains_v, mine, shares, slots, wgs, wus, wds, every,
    part, xs, ys, backs, first, second, row_in, plane_in, gs, gr, zs, zr, bs, br, ps, pr, cs, cr, ds, dr, ss, sr, ws,
    wr, local
):
    side, level = lax.axis_index("side"), lax.axis_index("lane")
    col, core = side // 2, side % 2
    mid = ((level + 1) // 2) % 2
    rows = out.shape[0]
    width = out.shape[1]
    chips = shares.shape[0]
    columns = chips // levels
    cap = xs.shape[1] // columns
    main = rows - spare
    cut = (main // 2 + 15) // 16 * 16
    bcut = spare // 2
    whole = (pl.ds(0, rows // 2), pl.ds(rows // 2, rows // 2))
    part_rows = (pl.ds(0, cut), pl.ds(cut, main - cut))
    tail_rows = (pl.ds(main, bcut), pl.ds(main + bcut, spare - bcut))
    tail = pl.ds(main, spare)
    dev_x, dev_y = (flip(col, 1) * 2 + core, level), (flip(col, 2) * 2 + core, level)
    twin = (col * 2 + 1 - core, level)
    mate = (side, flip(level, 1))
    inner = (side, mid * flip(level, 3) + (1 - mid) * flip(level, 1))
    lev = [
        level,
        flip(level, 1),
        mid * flip(level, 3) + (1 - mid) * flip(level, 2),
        mid * flip(level, 2) + (1 - mid) * flip(level, 3),
    ]
    me = col * levels + level
    others = [(flip(col, m // levels), flip(level, m % levels)) for m in range(1, chips)]

    fetch = [pltpu.make_async_copy(ids, ids_v, local.at[0]), pltpu.make_async_copy(gains, gains_v, local.at[1])]
    for copy in fetch:
        copy.start()
    barrier = pltpu.get_barrier_semaphore()
    friends = [(q * 2 + core, z) for q, z in others] + [twin]
    for device in friends:
        pl.semaphore_signal(barrier, inc=1, device_id=device, device_id_type=MESH)
    keep = [
        pltpu.make_async_copy(tokens, every.at[0, 0], local.at[2]),
        pltpu.make_async_copy(wg.at[0], wgs.at[0], local.at[3]),
        pltpu.make_async_copy(wu.at[0], wus.at[0], local.at[4]),
        pltpu.make_async_copy(wd.at[0], wds.at[0], local.at[5]),
    ]
    for copy in keep:
        copy.start()
    for copy in fetch:
        copy.wait()
    number = lax.broadcasted_iota(jnp.int32, (rows, 128), 1)
    table = jnp.zeros((rows, 128), F32)
    for k in range(ids_v.shape[1]):
        table = table + jnp.where(ids_v[:, k : k + 1] == number, gains_v[:, k : k + 1], 0.0)
    table = table.T
    for q in range(columns):
        for z in range(levels):
            for c in range(2):
                e = (q * 2 + c) * levels + z
                mine[q * levels + z, c : c + 1, :] = table[e : e + 1, :]
            mine[q * levels + z, 2:8, :] = jnp.zeros((6, rows), F32)
    shares[me] = mine[me]
    pl.semaphore_wait(barrier, len(friends))

    def link(src, dst, s, r, device):
        return pltpu.make_async_remote_copy(
            src_ref=src, dst_ref=dst, send_sem=s, recv_sem=r, device_id=device, device_id_type=MESH
        )

    def on_mid(do):
        pl.when(mid == 1)(do)

    def on_end(do):
        pl.when(mid == 0)(do)

    def spread_copies(k):
        p, q = whole if k == 0 else part_rows
        block = tokens if k == 0 else every.at[k, 0]
        return [
            link(block.at[p], every.at[k, 1, p], gs.at[k, 0], gr.at[k, 0], dev_x),
            link(block.at[q], every.at[k, 2, q], gs.at[k, 1], gr.at[k, 1], dev_y),
            link(block.at[q], every.at[k, 1, q], gs.at[k, 2], gr.at[k, 2], dev_x),
            link(block.at[p], every.at[k, 2, p], gs.at[k, 3], gr.at[k, 3], dev_y),
            link(every.at[k, 1, p], every.at[k, 3, p], gs.at[k, 4], gr.at[k, 4], dev_y),
            link(every.at[k, 2, q], every.at[k, 3, q], gs.at[k, 5], gr.at[k, 5], dev_x),
        ]

    spread = [spread_copies(k) for k in range(levels)]

    def spread_send(k):
        for i in range(4):
            spread[k][i].start()

    def spread_relay(k):
        spread[k][0].wait_recv()
        spread[k][4].start()
        spread[k][1].wait_recv()
        spread[k][5].start()

    def spread_done(k):
        for i in range(2, 6):
            spread[k][i].wait_recv()

    def line_copies(view, own, s, r):
        return [
            link(own, view(1), s.at[0], r.at[1], mate),
            link(own, view(2), s.at[1], r.at[2], inner),
            link(view(1), view(3), s.at[2], r.at[3], inner),
            link(view(2), view(2), s.at[3], r.at[2], mate),
            link(view(3), view(3), s.at[4], r.at[3], mate),
        ]

    lines = line_copies(lambda k: every.at[k, 0], tokens, zs, zr)

    def tails(k):
        return every.at[k, pl.ds(1, columns - 1), tail]

    bands = line_copies(tails, tails(0), bs, br)

    def line_wait(copies, k):
        copies[(0, 0, 1, 2)[k]].wait_recv()

    def line_send(copies):
        copies[0].start()
        on_mid(copies[1].start)

    def line_relay(copies, k):
        line_wait(copies, k)
        copies[k + 1].start()

    small = [
        link(mine.at[q * levels + z], shares.at[me], ss.at[i], sr.at[i], (q * 2 + core, z))
        for i, (q, z) in enumerate(others)
    ]
    swap = [
        link(wg.at[0], wgs.at[1], ws.at[0], wr.at[0], twin),
        link(wu.at[0], wus.at[1], ws.at[1], wr.at[1], twin),
        link(wd.at[0], wds.at[1], ws.at[2], wr.at[2], twin),
    ]

    def make_slots():
        chosen = (shares[...] > 0.0).astype(F32).astype(BF16).reshape(chips * 8, rows)
        before = lax.broadcasted_iota(jnp.int32, (rows, rows), 0) < lax.broadcasted_iota(
            jnp.int32, (rows, rows), 1
        )
        before = before.astype(F32).astype(BF16)
        slots[...] = jnp.dot(chosen, before, preferred_element_type=F32).reshape(chips, 8, rows)

    def compute(k, middle):
        place = lax.broadcasted_iota(jnp.int32, (cap, rows), 0).astype(F32)

        def pick(r, carry):
            b = (((col // 2 + r // 2) % 2) * 2 + (col + r) % 2) * levels + lev[k]
            gain, slot = shares[b], slots[b]
            wanted = []
            for e in range(2):
                g = jnp.where(core == 0, gain[e : e + 1], gain[1 - e : 2 - e])
                s = jnp.where(core == 0, slot[e : e + 1], slot[1 - e : 2 - e])
                wanted.append(jnp.where(s == place, g, 0.0))
            weights = jnp.concatenate(wanted, axis=0)
            chosen = jnp.where(weights > 0.0, 1.0, 0.0).astype(BF16)
            backs[r] = weights.T.astype(BF16)
            picked = jnp.dot(chosen, every[k, r], preferred_element_type=F32).astype(BF16)
            at = pl.ds(pl.multiple_of(r * cap, cap), cap)
            for e in range(2):
                xs[e, at] = picked[e * cap : (e + 1) * cap]
            return carry

        lax.fori_loop(0, columns, pick, 0)

        def expert(e, carry):
            @pl.when(e == 1)
            def _():
                middle()

            x = xs[e]
            gate = jnp.dot(x, wgs[e], preferred_element_type=F32)
            upper = jnp.dot(x, wus[e], preferred_element_type=F32)
            hidden = (gate / (1.0 + jnp.exp(-gate)) * upper).astype(BF16)
            ys[e] = jnp.dot(hidden, wds[e], preferred_element_type=F32).astype(BF16)
            return carry

        lax.fori_loop(0, 2, expert, 0)

        def mix(r, carry):
            at = pl.ds(pl.multiple_of(r * cap, cap), cap)
            y = jnp.concatenate([ys[e, at] for e in range(2)], axis=0)
            part[k, r] = jnp.dot(backs[r], y, preferred_element_type=F32).astype(BF16)
            return carry

        lax.fori_loop(0, columns, mix, 0)

    def fold_copies(g):
        k = g % levels
        p, q = part_rows if g < levels else tail_rows
        a, b = pl.ds(0, p.size), pl.ds(0, q.size)
        return [
            link(part.at[k, 3, p], first.at[g, 0, a], ps.at[g, 0], pr.at[g, 0], dev_x),
            link(part.at[k, 3, q], first.at[g, 1, b], ps.at[g, 1], pr.at[g, 1], dev_y),
            link(part.at[k, 1, p], first.at[g, 2, a], ps.at[g, 2], pr.at[g, 2], dev_x),
            link(part.at[k, 2, q], first.at[g, 3, b], ps.at[g, 3], pr.at[g, 3], dev_y),
            link(part.at[k, 2, p], second.at[g, 0, a], ps.at[g, 4], pr.at[g, 4], dev_y),
            link(part.at[k, 1, q], second.at[g, 1, b], ps.at[g, 5], pr.at[g, 5], dev_x),
        ]

    folds = [fold_copies(g) for g in range(levels + 1)]

    def fold_one(g):
        for i in range(4):
            folds[g][i].start()

    def fold_two(g):
        k = g % levels
        p, q = part_rows if g < levels else tail_rows
        for i, (r, piece) in enumerate(((2, p), (1, q))):
            folds[g][i].wait_recv()
            part[k, r, piece] = (
                part[k, r, piece].astype(F32) + first[g, i, pl.ds(0, piece.size)].astype(F32)
            ).astype(BF16)
            folds[g][4 + i].start()

    def fold_sum(g, i):
        k = g % levels
        piece = (part_rows if g < levels else tail_rows)[i]
        at = pl.ds(0, piece.size)
        return (
            part[k, 0, piece].astype(F32) + first[g, 2 + i, at].astype(F32) + second[g, i, at].astype(F32)
        )

    def fold_three(g, store):
        for i in range(2):
            folds[g][2 + i].wait_recv()
            folds[g][4 + i].wait_recv()
            store(i, fold_sum(g, i))

    def keep_sum(k):
        def store(i, value):
            part[k, 0, part_rows[i]] = value.astype(BF16)

        return store

    def chain(view, land, s, r):
        send_end = {
            3: link(view(3), land.at[3], s.at[3], r.at[3], mate),
            2: link(view(2), land.at[2], s.at[2], r.at[2], mate),
            1: link(view(1), land.at[0], s.at[1], r.at[0], mate),
        }
        send_mid = {
            3: link(view(3), land.at[4], s.at[3], r.at[4], inner),
            2: link(view(2), land.at[1], s.at[2], r.at[1], inner),
            1: send_end[1],
        }
        return send_end, send_mid, {3: 3, 2: 2, 1: 4}

    def main_view(k):
        return part.at[k, 0, pl.ds(0, main)]

    def tail_view(k):
        return part.at[k, pl.ds(0, columns), tail]

    rows_chain = chain(main_view, row_in, cs, cr)
    tail_chain = chain(tail_view, plane_in, ds, dr)

    def landed(land, r, slot):
        link(land.at[slot], land.at[slot], r.at[slot], r.at[slot], mate).wait_recv()

    def chain_end(c, k):
        on_end(c[0][k].start)

    def chain_mid(c, view, land, r, k):
        def do():
            slot = c[2][k]
            landed(land, r, slot)
            here = view(k)
            here[...] = (here[...].astype(F32) + land[slot].astype(F32)).astype(BF16)
            c[1][k].start()

        on_mid(do)

    def main_end(k):
        chain_end(rows_chain, k)

    def main_mid(k):
        chain_mid(rows_chain, main_view, row_in, cr, k)

    def tail_end(k):
        chain_end(tail_chain, k)

    def tail_mid(k):
        chain_mid(tail_chain, tail_view, plane_in, dr, k)

    spread[0][0].start()
    spread[0][1].start()
    line_send(lines)
    for copy in small:
        copy.start()
    spread[0][2].start()
    spread[0][3].start()
    for copy in swap:
        copy.start()
    spread_relay(0)
    line_wait(lines, 1)
    on_mid(lines[2].start)
    spread_send(1)
    on_mid(lambda: line_relay(lines, 2))
    for copy in small:
        copy.wait_recv()
    make_slots()
    spread_done(0)
    line_send(bands)
    for copy in keep:
        copy.wait()

    def hook_0():
        spread_relay(1)
        on_mid(lambda: line_relay(lines, 3))
        for copy in swap:
            copy.wait_recv()

    compute(0, hook_0)
    on_end(lambda: line_wait(lines, 2))
    spread_send(2)
    line_wait(bands, 1)
    on_mid(bands[2].start)
    spread_done(1)

    def hook_1():
        spread_relay(2)
        on_mid(lambda: line_relay(bands, 2))

    compute(1, hook_1)
    tail_end(1)
    on_end(lambda: line_wait(lines, 3))
    spread_send(3)
    on_mid(lambda: line_relay(bands, 3))
    spread_done(2)
    on_end(lambda: line_wait(bands, 2))

    def hook_2():
        spread_relay(3)
        fold_one(1)

    compute(2, hook_2)
    tail_end(2)
    spread_done(3)
    on_end(lambda: line_wait(bands, 3))

    def hook_3():
        fold_two(1)

    compute(3, hook_3)
    fold_one(3)
    tail_end(3)
    fold_two(3)
    tail_mid(2)
    fold_one(2)
    fold_three(3, keep_sum(3))
    main_end(3)
    tail_mid(3)
    fold_three(1, keep_sum(1))
    main_end(1)
    fold_two(2)
    fold_one(0)
    main_mid(3)
    fold_three(2, keep_sum(2))
    main_end(2)
    tail_mid(1)
    fold_two(0)
    main_mid(2)
    landed(plane_in, dr, 0)
    on_mid(lambda: landed(plane_in, dr, 1))

    def own(land, extra):
        return land[0].astype(F32) + jnp.where(mid == 1, land[1].astype(F32), 0.0)

    for r in range(columns):
        part[0, r, tail] = (part[0, r, tail].astype(F32) + own(plane_in.at[:, r], r)).astype(BF16)
    fold_one(levels)
    main_mid(1)
    fold_two(levels)
    landed(row_in, cr, 0)
    on_mid(lambda: landed(row_in, cr, 1))

    def main_out(i, value):
        piece = part_rows[i]
        total = value + row_in[0, piece].astype(F32) + jnp.where(mid == 1, row_in[1, piece].astype(F32), 0.0)
        out[piece] = total.astype(BF16)

    def tail_out(i, value):
        out[tail_rows[i]] = value.astype(BF16)

    fold_three(0, main_out)
    fold_three(levels, tail_out)

    for group in spread + folds + [small, swap]:
        for copy in group:
            copy.wait_send()
    for copies in (lines, bands):
        copies[0].wait_send()
    for c in (rows_chain, tail_chain):
        c[0][1].wait_send()

    @pl.when(mid == 1)
    def _():
        for copies in (lines, bands):
            for copy in copies[1:]:
                copy.wait_send()
        for c in (rows_chain, tail_chain):
            c[1][2].wait_send()
            c[1][3].wait_send()

    @pl.when(mid == 0)
    def _():
        for c in (rows_chain, tail_chain):
            c[0][2].wait_send()
            c[0][3].wait_send()


def on_layers(levels, tokens, expert_ids, route_weights, w_gate, w_up, w_down):
    tok_rows, width = tokens.shape
    top_count = expert_ids.shape[1]
    device_count = lax.axis_size("side") * levels
    capacity = 2 * tok_rows * top_count // device_count
    chips = device_count // 2
    columns = chips // levels
    spare = tok_rows // 4
    main = tok_rows - spare
    cut = (main // 2 + 15) // 16 * 16
    anywhere = pl.BlockSpec(memory_space=pl.ANY)
    vmem = pltpu.VMEM
    dma = pltpu.SemaphoreType.DMA
    return pl.pallas_call(
        functools.partial(fused_kernel, levels, spare),
        out_shape=jax.ShapeDtypeStruct((tok_rows, width), BF16),
        in_specs=[anywhere] * 6,
        out_specs=pl.BlockSpec(memory_space=vmem),
        scratch_shapes=[
            vmem(expert_ids.shape, jnp.int32),
            vmem(route_weights.shape, F32),
            vmem((chips, 8, tok_rows), F32),
            vmem((chips, 8, tok_rows), F32),
            vmem((chips, 8, tok_rows), F32),
            vmem((2,) + w_gate.shape[1:], BF16),
            vmem((2,) + w_up.shape[1:], BF16),
            vmem((2,) + w_down.shape[1:], BF16),
            vmem((levels, columns, tok_rows, width), BF16),
            vmem((levels, columns, tok_rows, width), BF16),
            vmem((2, columns * capacity, width), BF16),
            vmem((2, columns * capacity, width), BF16),
            vmem((columns, tok_rows, 2 * capacity), BF16),
            vmem((levels + 1, 4, cut, width), BF16),
            vmem((levels + 1, 2, cut, width), BF16),
            vmem((5, main, width), BF16),
            vmem((5, columns, spare, width), BF16),
            dma((levels, 6)),
            dma((levels, 6)),
            dma((5,)),
            dma((4,)),
            dma((5,)),
            dma((4,)),
            dma((levels + 1, 6)),
            dma((levels + 1, 6)),
            dma((4,)),
            dma((5,)),
            dma((4,)),
            dma((5,)),
            dma((chips - 1,)),
            dma((chips - 1,)),
            dma((3,)),
            dma((3,)),
            dma((6,)),
        ],
        compiler_params=pltpu.CompilerParams(
            collective_id=0, has_side_effects=True, vmem_limit_bytes=62 * 2**20
        ),
        name="layer",
    )(tokens, expert_ids, route_weights, w_gate, w_up, w_down)


def expert_ffn(rows, gate_proj, up_proj, down_proj):
    gate = jnp.dot(rows, gate_proj, preferred_element_type=jnp.float32)
    upper = jnp.dot(rows, up_proj, preferred_element_type=jnp.float32)
    hidden = (jax.nn.silu(gate) * upper).astype(jnp.bfloat16)
    return jnp.dot(hidden, down_proj, preferred_element_type=jnp.float32).astype(jnp.bfloat16)


def on_device(tokens, expert_ids, route_weights, w_gate, w_up, w_down):
    tok_rows = tokens.shape[0]
    width = tokens.shape[1]
    top_count = expert_ids.shape[1]
    side_count = lax.axis_size("side")
    device_count = side_count * lax.axis_size("lane")
    local_count = w_gate.shape[0]
    expert_count = device_count * local_count
    capacity = 2 * tok_rows * top_count // expert_count
    flat_ids = expert_ids.reshape(-1)
    onehot = (flat_ids[:, None] == jnp.arange(expert_count, dtype=jnp.int32)[None, :]).astype(
        jnp.int32
    )
    earlier = jnp.cumsum(onehot, axis=0) - onehot
    slot_index = jnp.sum(earlier * onehot, axis=1)
    position = (flat_ids * capacity + slot_index).reshape(tok_rows, top_count)
    buffer_rows = jnp.arange(expert_count * capacity, dtype=jnp.int32)
    dispatch_table = jnp.any(buffer_rows[:, None, None] == position[None, :, :], axis=2).astype(
        jnp.bfloat16
    )
    outgoing = jnp.dot(dispatch_table, tokens, preferred_element_type=jnp.float32).astype(
        jnp.bfloat16
    )
    outgoing = outgoing.reshape(expert_count, capacity, width)
    received = lax.all_to_all(outgoing, ("side", "lane"), split_axis=0, concat_axis=0, tiled=True)
    count = received.shape[1]
    grouped = received.reshape(device_count, local_count, count, width)
    rows = grouped[:, 0].reshape(device_count * count, width)
    output = expert_ffn(rows, w_gate[0], w_up[0], w_down[0])
    results = [output.reshape(device_count, count, width)]
    returned = lax.all_to_all(
        jnp.stack(results, axis=1).reshape(device_count * local_count, count, width),
        ("side", "lane"),
        split_axis=0,
        concat_axis=0,
        tiled=True,
    )
    flat_back = returned.reshape(expert_count * capacity, width)
    picked = flat_back[position]
    mixed = jnp.einsum("tk,tkd->td", route_weights, picked, preferred_element_type=jnp.float32)
    return mixed.astype(jnp.bfloat16)


def layered(mesh, tokens):
    side, levels = mesh.shape["side"], mesh.shape["lane"]
    layer_bytes = tokens.shape[0] // 2 * tokens.shape[1] * tokens.dtype.itemsize
    fits = 3 * layer_bytes < 32 * 2**20 and side * levels <= tokens.shape[0] // (side * levels) == 2**7
    return side == 2**3 and levels == 4 and fits


def solution(mesh):
    placed = (
        P(AXES, None),
        P(AXES, None),
        P(AXES, None),
        P(AXES, None, None),
        P(AXES, None, None),
        P(AXES, None, None),
    )

    def run(tokens, *rest):
        body = on_device
        if layered(mesh, tokens):
            body = functools.partial(on_layers, mesh.shape["lane"])
        return jax.shard_map(
            body, mesh=mesh, in_specs=placed, out_specs=P(AXES, None), check_vma=False
        )(tokens, *rest)

    return run
```

time: 190 us -> 132 us (0.69)
  Pallas kernels: 181 us -> 127 us
  other arithmetic: 2.89 us -> 0 us
    pallas_call x2 -> x1, Pallas kernels: 181 us -> 127 us  [on_layers(): pl.pallas_call(functools.partial(fused_kernel, levels, spare), out_shape=...]
    unnamed x1 -> x3, local copies, waits for them, and re-layouts: 1.88 us -> 4.7 us
where the time goes in v1:
time: 132 us
  Pallas kernels  127 us (96%)
  local copies, waits for them, and re-layouts  4.7 us (4%)
    pallas_call x1, Pallas kernels, on_layers(): pl.pallas_call(functools.partial(fused_kernel, levels, spare), out_shape=...  127 us
    unnamed x3, local copies, waits for them, and re-layouts  4.7 us

profile of v1, /device:TPU:0, one launch (start us, length us, event | category | flops | bytes accessed | tf_op | source)
XLA Modules:
  0.0 132.2 jit_solution(5480765741704745052)
XLA Ops:
  0.0 1.4 %copy.7.ids = s32[128,8]{1,0:T(8,128)} copy(s32[128,8]{0,1:T(8,128)} %param.7) | data formatting | bytes 8192 | tf_op args[1]
  1.4 1.4 %copy.8.gains = f32[128,8]{1,0:T(8,128)} copy(f32[128,8]{0,1:T(8,128)} %param.8) | data formatting | bytes 8192 | tf_op args[2]
  2.8 127.4 %layer.1 = bf16[128,2048]{1,0:T(8,128)(2,1)} custom-call(bf16[128,2048]{1,0:T(8,128)(2,1)} %tokens.1, s32[128,8]{1,0:T(8,128)} %copy.7.ids, f32[128,8]{1,0:T(8,128)} %copy.8.gains, bf16[1,2048,768]{2,1,0:T(8,128)(2,1)} %wg.1, bf16[1,2048,768]{2,1,0:T(8,128)(2,1)} %wu.1, bf16[1,768,2048]{2,1,0:T(8,128)(2,1)} %wd.1), custom_call_target="tpu_custom_call" | custom-call | tf_op jit(solution)/shard_map/layer/pallas_call | solution.py:457
  130.3 1.9 %copy.10 = bf16[128,2048]{1,0:T(8,128)(2,1)} copy(bf16[128,2048]{1,0:T(8,128)(2,1)} %layer.1) | data formatting | bytes 1048576

commit v2 on v1

--- a/solution.py
+++ b/solution.py
@@ -11,6 +11,48 @@
 MESH = pl.DeviceIdType.MESH
 BF16 = jnp.bfloat16
 F32 = jnp.float32
+
+
+ORDER = [
+    ("all", "Start"), ("end", "Sr", 0), ("end", "Lw", 1), ("end", "Ss", 1), ("end", "T"),
+    ("end", "Sd", 0), ("end", "Bs"), ("mid", "Sr", 0), ("mid", "Lr", 2, 0), ("mid", "Lr", 1, 0),
+    ("mid", "Lr", 2, 1), ("mid", "Ss", 2), ("mid", "Lr", 1, 1), ("mid", "Sd", 0), ("mid", "T"),
+    ("mid", "Ss", 1), ("mid", "Bs"), ("mid", "Bi"), ("mid", "Br", 1, 0), ("mid", "Lr", 3, 1),
+    ("mid", "Lr", 3, 0), ("mid", "Sr", 1),
+    ("all", "C", 0, [
+        ("end", "Sr", 1), ("end", "Lw", 2), ("mid", "Sr", 2), ("mid", "Ss", 3), ("mid", "Br", 2, 1),
+        ("all", "Swap"),
+    ]),
+    ("end", "Ss", 2), ("end", "Bw", 1), ("end", "Sd", 1), ("end", "Sr", 2), ("mid", "Br", 2, 0),
+    ("mid", "Sd", 1), ("mid", "Br", 1, 1),
+    ("all", "C", 1, [
+        ("mid", "Br", 3, 0), ("mid", "Br", 3, 1),
+    ]),
+    ("end", "Lw", 3), ("end", "Ss", 3), ("end", "De", 1, 0), ("end", "De", 1, 1), ("end", "Bw", 2),
+    ("end", "Sr", 3), ("end", "Sd", 2), ("end", "F1", 1), ("mid", "Sr", 3), ("mid", "F1", 1),
+    ("mid", "Sd", 2),
+    ("all", "C", 2, [
+        ("mid", "F2", 1), ("mid", "Sd", 3),
+    ]),
+    ("end", "Sd", 3), ("end", "De", 2, 0), ("end", "De", 2, 1), ("end", "Bw", 3), ("mid", "F1", 2),
+    ("all", "C", 3, [
+        ("end", "F2", 1), ("mid", "Dm", 2, 0),
+    ]),
+    ("end", "De", 3, 0), ("end", "F1", 3), ("end", "De", 3, 1), ("end", "F2", 3), ("end", "F1", 2),
+    ("end", "F3", 3, 0), ("end", "Ce", 3, 0), ("end", "F3", 1, 0), ("end", "F3", 1, 1),
+    ("end", "F3", 3, 1), ("end", "Ce", 3, 1), ("end", "F2", 2), ("end", "F1", 0), ("end", "Ce", 1, 0),
+    ("end", "Dw", 0), ("end", "F3", 2, 0), ("end", "Ce", 2, 0), ("end", "F3", 2, 1),
+    ("end", "Ce", 2, 1), ("end", "Dw", 1), ("end", "F1", 4), ("end", "Ce", 1, 1), ("end", "F2", 0),
+    ("end", "Cw", 1), ("end", "F2", 4), ("end", "F3", 0, 0), ("end", "Cw", 0), ("end", "F3", 0, 1),
+    ("end", "F3", 4, 0), ("end", "F3", 4, 1), ("mid", "F1", 3), ("mid", "Dm", 2, 1),
+    ("mid", "Dm", 3, 0), ("mid", "F3", 1, 0), ("mid", "Dw", 0), ("mid", "F2", 3), ("mid", "Dm", 3, 1),
+    ("mid", "Dw", 1), ("mid", "F1", 4), ("mid", "Dm", 1, 0), ("mid", "F3", 1, 1), ("mid", "F2", 2),
+    ("mid", "F3", 3, 1), ("mid", "F3", 3, 0), ("mid", "Dm", 1, 1), ("mid", "Cm", 3, 1),
+    ("mid", "F1", 0), ("mid", "Cm", 3, 0), ("mid", "F2", 4), ("mid", "F3", 2, 0), ("mid", "F2", 0),
+    ("mid", "Cm", 1, 1), ("mid", "Cm", 2, 0), ("mid", "Cm", 1, 0), ("mid", "F3", 2, 1),
+    ("mid", "Cm", 2, 1), ("mid", "F3", 4, 0), ("mid", "F3", 4, 1), ("mid", "F3", 0, 1),
+    ("mid", "Cw", 0), ("mid", "F3", 0, 0), ("mid", "Cw", 1),
+]
 
 
 def flip(value, mask):
@@ -42,7 +84,6 @@
     whole = (pl.ds(0, rows // 2), pl.ds(rows // 2, rows // 2))
     part_rows = (pl.ds(0, cut), pl.ds(cut, main - cut))
     tail_rows = (pl.ds(main, bcut), pl.ds(main + bcut, spare - bcut))
-    tail = pl.ds(main, spare)
     dev_x, dev_y = (flip(col, 1) * 2 + core, level), (flip(col, 2) * 2 + core, level)
     twin = (col * 2 + 1 - core, level)
     mate = (side, flip(level, 1))
@@ -73,11 +114,10 @@
         copy.start()
     for copy in fetch:
         copy.wait()
-    number = lax.broadcasted_iota(jnp.int32, (rows, 128), 1)
-    table = jnp.zeros((rows, 128), F32)
-    for k in range(ids_v.shape[1]):
-        table = table + jnp.where(ids_v[:, k : k + 1] == number, gains_v[:, k : k + 1], 0.0)
-    table = table.T
+    number = lax.broadcasted_iota(jnp.int32, (2 * chips, rows), 0)
+    table = jnp.zeros((2 * chips, rows), F32)
+    for k in range(ids_v.shape[0]):
+        table = table + jnp.where(ids_v[k : k + 1] == number, gains_v[k : k + 1], 0.0)
     for q in range(columns):
         for z in range(levels):
             for c in range(2):
@@ -127,31 +167,44 @@
             spread[k][i].wait_recv()
 
     def line_copies(view, own, s, r):
-        return [
-            link(own, view(1), s.at[0], r.at[1], mate),
-            link(own, view(2), s.at[1], r.at[2], inner),
-            link(view(1), view(3), s.at[2], r.at[3], inner),
-            link(view(2), view(2), s.at[3], r.at[2], mate),
-            link(view(3), view(3), s.at[4], r.at[3], mate),
-        ]
-
-    lines = line_copies(lambda k: every.at[k, 0], tokens, zs, zr)
-
-    def tails(k):
-        return every.at[k, pl.ds(1, columns - 1), tail]
-
-    bands = line_copies(tails, tails(0), bs, br)
+        out = []
+        for i in range(2):
+            out.append(
+                [
+                    link(own(i), view(1, i), s.at[0, i], r.at[1, i], mate),
+                    link(own(i), view(2, i), s.at[1, i], r.at[2, i], inner),
+                    link(view(1, i), view(3, i), s.at[2, i], r.at[3, i], inner),
+                    link(view(2, i), view(2, i), s.at[3, i], r.at[2, i], mate),
+                    link(view(3, i), view(3, i), s.at[4, i], r.at[3, i], mate),
+                ]
+            )
+        return out
+
+    block_rows = (pl.ds(0, cut), pl.ds(cut, rows - cut))
+    lines = line_copies(
+        lambda k, i: every.at[k, 0, block_rows[i]], lambda i: tokens.at[block_rows[i]], zs, zr
+    )
+
+    def tails(k, i):
+        return every.at[k, pl.ds(1, columns - 1), tail_rows[i]]
+
+    bands = line_copies(tails, lambda i: tails(0, i), bs, br)
+
+    def line_send(copies):
+        for i in range(2):
+            copies[i][0].start()
+
+    def line_send_inner(copies):
+        for i in range(2):
+            copies[i][1].start()
 
     def line_wait(copies, k):
-        copies[(0, 0, 1, 2)[k]].wait_recv()
-
-    def line_send(copies):
-        copies[0].start()
-        on_mid(copies[1].start)
-
-    def line_relay(copies, k):
-        line_wait(copies, k)
-        copies[k + 1].start()
+        for i in range(2):
+            copies[i][k - 1].wait_recv()
+
+    def line_relay(copies, k, i):
+        copies[i][k - 1].wait_recv()
+        copies[i][k + 1].start()
 
     small = [
         link(mine.at[q * levels + z], shares.at[me], ss.at[i], sr.at[i], (q * 2 + core, z))
@@ -244,6 +297,10 @@
             ).astype(BF16)
             folds[g][4 + i].start()
 
+    def fold_wait(g, i):
+        folds[g][2 + i].wait_recv()
+        folds[g][4 + i].wait_recv()
+
     def fold_sum(g, i):
         k = g % levels
         piece = (part_rows if g < levels else tail_rows)[i]
@@ -252,193 +309,154 @@
             part[k, 0, piece].astype(F32) + first[g, 2 + i, at].astype(F32) + second[g, i, at].astype(F32)
         )
 
-    def fold_three(g, store):
-        for i in range(2):
-            folds[g][2 + i].wait_recv()
-            folds[g][4 + i].wait_recv()
-            store(i, fold_sum(g, i))
-
-    def keep_sum(k):
-        def store(i, value):
-            part[k, 0, part_rows[i]] = value.astype(BF16)
-
-        return store
+    def fold_three(g, i):
+        fold_wait(g, i)
+        if g == levels:
+            out[tail_rows[i]] = fold_sum(g, i).astype(BF16)
+        elif g:
+            part[g, 0, part_rows[i]] = fold_sum(g, i).astype(BF16)
 
     def chain(view, land, s, r):
-        send_end = {
-            3: link(view(3), land.at[3], s.at[3], r.at[3], mate),
-            2: link(view(2), land.at[2], s.at[2], r.at[2], mate),
-            1: link(view(1), land.at[0], s.at[1], r.at[0], mate),
-        }
-        send_mid = {
-            3: link(view(3), land.at[4], s.at[3], r.at[4], inner),
-            2: link(view(2), land.at[1], s.at[2], r.at[1], inner),
-            1: send_end[1],
-        }
-        return send_end, send_mid, {3: 3, 2: 2, 1: 4}
-
-    def main_view(k):
-        return part.at[k, 0, pl.ds(0, main)]
-
-    def tail_view(k):
-        return part.at[k, pl.ds(0, columns), tail]
-
-    rows_chain = chain(main_view, row_in, cs, cr)
-    tail_chain = chain(tail_view, plane_in, ds, dr)
-
-    def landed(land, r, slot):
-        link(land.at[slot], land.at[slot], r.at[slot], r.at[slot], mate).wait_recv()
-
-    def chain_end(c, k):
-        on_end(c[0][k].start)
-
-    def chain_mid(c, view, land, r, k):
-        def do():
-            slot = c[2][k]
-            landed(land, r, slot)
-            here = view(k)
-            here[...] = (here[...].astype(F32) + land[slot].astype(F32)).astype(BF16)
-            c[1][k].start()
-
-        on_mid(do)
-
-    def main_end(k):
-        chain_end(rows_chain, k)
-
-    def main_mid(k):
-        chain_mid(rows_chain, main_view, row_in, cr, k)
-
-    def tail_end(k):
-        chain_end(tail_chain, k)
-
-    def tail_mid(k):
-        chain_mid(tail_chain, tail_view, plane_in, dr, k)
-
-    spread[0][0].start()
-    spread[0][1].start()
-    line_send(lines)
-    for copy in small:
-        copy.start()
-    spread[0][2].start()
-    spread[0][3].start()
-    for copy in swap:
-        copy.start()
-    spread_relay(0)
-    line_wait(lines, 1)
-    on_mid(lines[2].start)
-    spread_send(1)
-    on_mid(lambda: line_relay(lines, 2))
-    for copy in small:
-        copy.wait_recv()
-    make_slots()
-    spread_done(0)
-    line_send(bands)
-    for copy in keep:
-        copy.wait()
-
-    def hook_0():
-        spread_relay(1)
-        on_mid(lambda: line_relay(lines, 3))
+        send_end, send_mid = {}, {}
+        for i in range(2):
+            for k, end_slot, mid_slot in ((3, 3, 4), (2, 2, 1), (1, 0, 0)):
+                send_end[k, i] = link(view(k, i), land(end_slot, i), s.at[k, i], r.at[end_slot, i], mate)
+                send_mid[k, i] = link(
+                    view(k, i), land(mid_slot, i), s.at[k, i], r.at[mid_slot, i], mate if k == 1 else inner
+                )
+        return send_end, send_mid, view, land, r
+
+    def main_view(k, i):
+        return part.at[k, 0, part_rows[i]]
+
+    def tail_view(k, i):
+        return part.at[k, pl.ds(0, columns), tail_rows[i]]
+
+    rows_chain = chain(main_view, lambda slot, i: row_in.at[slot, part_rows[i]], cs, cr)
+    tail_chain = chain(
+        tail_view,
+        lambda slot, i: plane_in.at[slot, pl.ds(0, columns), (pl.ds(0, bcut), pl.ds(bcut, spare - bcut))[i]],
+        ds,
+        dr,
+    )
+
+    def landed(c, slot, i):
+        land, r = c[3], c[4]
+        link(land(slot, i), land(slot, i), r.at[slot, i], r.at[slot, i], mate).wait_recv()
+
+    def chain_mid(c, k, i):
+        slot = {3: 3, 2: 2, 1: 4}[k]
+        landed(c, slot, i)
+        here = c[2](k, i)
+        here[...] = (here[...].astype(F32) + c[3](slot, i)[...].astype(F32)).astype(BF16)
+        c[1][k, i].start()
+
+    def own_wait(c, i):
+        landed(c, 0, i)
+
+        @pl.when(mid == 1)
+        def _():
+            landed(c, 1, i)
+
+    def own_rows(c, i):
+        return c[3](0, i)[...].astype(F32) + jnp.where(mid == 1, c[3](1, i)[...].astype(F32), 0.0)
+
+    def own_tail(i):
+        own_wait(tail_chain, i)
+        here = tail_view(0, i)
+        here[...] = (here[...].astype(F32) + own_rows(tail_chain, i)).astype(BF16)
+
+    def first_send():
+        spread[0][0].start()
+        spread[0][1].start()
+        line_send(lines)
+        on_mid(lambda: line_send_inner(lines))
+        for copy in small:
+            copy.start()
+        spread[0][2].start()
+        spread[0][3].start()
+        for copy in swap:
+            copy.start()
+
+    def make_tables():
+        for copy in small:
+            copy.wait_recv()
+        make_slots()
+        for copy in keep:
+            copy.wait()
+
+    def swapped():
         for copy in swap:
             copy.wait_recv()
 
-    compute(0, hook_0)
-    on_end(lambda: line_wait(lines, 2))
-    spread_send(2)
-    line_wait(bands, 1)
-    on_mid(bands[2].start)
-    spread_done(1)
-
-    def hook_1():
-        spread_relay(2)
-        on_mid(lambda: line_relay(bands, 2))
-
-    compute(1, hook_1)
-    tail_end(1)
-    on_end(lambda: line_wait(lines, 3))
-    spread_send(3)
-    on_mid(lambda: line_relay(bands, 3))
-    spread_done(2)
-    on_end(lambda: line_wait(bands, 2))
-
-    def hook_2():
-        spread_relay(3)
-        fold_one(1)
-
-    compute(2, hook_2)
-    tail_end(2)
-    spread_done(3)
-    on_end(lambda: line_wait(bands, 3))
-
-    def hook_3():
-        fold_two(1)
-
-    compute(3, hook_3)
-    fold_one(3)
-    tail_end(3)
-    fold_two(3)
-    tail_mid(2)
-    fold_one(2)
-    fold_three(3, keep_sum(3))
-    main_end(3)
-    tail_mid(3)
-    fold_three(1, keep_sum(1))
-    main_end(1)
-    fold_two(2)
-    fold_one(0)
-    main_mid(3)
-    fold_three(2, keep_sum(2))
-    main_end(2)
-    tail_mid(1)
-    fold_two(0)
-    main_mid(2)
-    landed(plane_in, dr, 0)
-    on_mid(lambda: landed(plane_in, dr, 1))
-
-    def own(land, extra):
-        return land[0].astype(F32) + jnp.where(mid == 1, land[1].astype(F32), 0.0)
-
-    for r in range(columns):
-        part[0, r, tail] = (part[0, r, tail].astype(F32) + own(plane_in.at[:, r], r)).astype(BF16)
-    fold_one(levels)
-    main_mid(1)
-    fold_two(levels)
-    landed(row_in, cr, 0)
-    on_mid(lambda: landed(row_in, cr, 1))
-
-    def main_out(i, value):
-        piece = part_rows[i]
-        total = value + row_in[0, piece].astype(F32) + jnp.where(mid == 1, row_in[1, piece].astype(F32), 0.0)
-        out[piece] = total.astype(BF16)
-
-    def tail_out(i, value):
-        out[tail_rows[i]] = value.astype(BF16)
-
-    fold_three(0, main_out)
-    fold_three(levels, tail_out)
+    def run(events):
+        n = 0
+        while n < len(events):
+            who, stop = events[n][0], n + 1
+            while stop < len(events) and events[stop][0] == who:
+                stop += 1
+            group = events[n:stop]
+
+            def do(group=group):
+                for event in group:
+                    acts[event[1]](*event[2:])
+
+            {"all": lambda f: f(), "end": on_end, "mid": on_mid}[who](do)
+            n = stop
+
+    acts = {
+        "Start": first_send,
+        "T": make_tables,
+        "Swap": swapped,
+        "Ss": spread_send,
+        "Sr": spread_relay,
+        "Sd": spread_done,
+        "Lr": lambda k, i: line_relay(lines, k, i),
+        "Lw": lambda k: line_wait(lines, k),
+        "Bs": lambda: line_send(bands),
+        "Bi": lambda: line_send_inner(bands),
+        "Br": lambda k, i: line_relay(bands, k, i),
+        "Bw": lambda k: line_wait(bands, k),
+        "C": lambda k, hook: compute(k, lambda: run(hook)),
+        "F1": fold_one,
+        "F2": fold_two,
+        "F3": fold_three,
+        "De": lambda k, i: tail_chain[0][k, i].start(),
+        "Dm": lambda k, i: chain_mid(tail_chain, k, i),
+        "Dw": own_tail,
+        "Ce": lambda k, i: rows_chain[0][k, i].start(),
+        "Cm": lambda k, i: chain_mid(rows_chain, k, i),
+        "Cw": lambda i: own_wait(rows_chain, i),
+    }
+    run(ORDER)
+    for i, piece in enumerate(part_rows):
+        out[piece] = (fold_sum(0, i) + own_rows(rows_chain, i)).astype(BF16)
 
     for group in spread + folds + [small, swap]:
         for copy in group:
             copy.wait_send()
-    for copies in (lines, bands):
-        copies[0].wait_send()
-    for c in (rows_chain, tail_chain):
-        c[0][1].wait_send()
+    for i in range(2):
+        for copies in (lines, bands):
+            copies[i][0].wait_send()
+        for c in (rows_chain, tail_chain):
+            c[0][1, i].wait_send()
 
     @pl.when(mid == 1)
     def _():
-        for copies in (lines, bands):
-            for copy in copies[1:]:
-                copy.wait_send()
-        for c in (rows_chain, tail_chain):
-            c[1][2].wait_send()
-            c[1][3].wait_send()
+        for i in range(2):
+            for copies in (lines, bands):
+                for copy in copies[i][1:]:
+                    copy.wait_send()
+            for c in (rows_chain, tail_chain):
+                c[1][2, i].wait_send()
+                c[1][3, i].wait_send()
 
     @pl.when(mid == 0)
     def _():
-        for c in (rows_chain, tail_chain):
-            c[0][2].wait_send()
-            c[0][3].wait_send()
+        for i in range(2):
+            for c in (rows_chain, tail_chain):
+                c[0][2, i].wait_send()
+                c[0][3, i].wait_send()
 
 
 def on_layers(levels, tokens, expert_ids, route_weights, w_gate, w_up, w_down):
@@ -460,8 +478,8 @@
         in_specs=[anywhere] * 6,
         out_specs=pl.BlockSpec(memory_space=vmem),
         scratch_shapes=[
-            vmem(expert_ids.shape, jnp.int32),
-            vmem(route_weights.shape, F32),
+            vmem((top_count, tok_rows), jnp.int32),
+            vmem((top_count, tok_rows), F32),
             vmem((chips, 8, tok_rows), F32),
             vmem((chips, 8, tok_rows), F32),
             vmem((chips, 8, tok_rows), F32),
@@ -479,16 +497,16 @@
             vmem((5, columns, spare, width), BF16),
             dma((levels, 6)),
             dma((levels, 6)),
-            dma((5,)),
-            dma((4,)),
-            dma((5,)),
-            dma((4,)),
+            dma((5, 2)),
+            dma((4, 2)),
+            dma((5, 2)),
+            dma((4, 2)),
             dma((levels + 1, 6)),
             dma((levels + 1, 6)),
-            dma((4,)),
-            dma((5,)),
-            dma((4,)),
-            dma((5,)),
+            dma((4, 2)),
+            dma((5, 2)),
+            dma((4, 2)),
+            dma((5, 2)),
             dma((chips - 1,)),
             dma((chips - 1,)),
             dma((3,)),
@@ -499,7 +517,7 @@
             collective_id=0, has_side_effects=True, vmem_limit_bytes=62 * 2**20
         ),
         name="layer",
-    )(tokens, expert_ids, route_weights, w_gate, w_up, w_down)
+    )(tokens, expert_ids.T, route_weights.T, w_gate, w_up, w_down)
 
 
 def expert_ffn(rows, gate_proj, up_proj, down_proj):

time: 132 us -> 125 us (0.947)
  Pallas kernels: 127 us -> 123 us
  local copies, waits for them, and re-layouts: 4.7 us -> 1.88 us
    pallas_call x1, Pallas kernels: 127 us -> 123 us  [on_layers(): pl.pallas_call(functools.partial(fused_kernel, levels, spare), out_shape=...]
    unnamed x3 -> x1, local copies, waits for them, and re-layouts: 4.7 us -> 1.88 us
where the time goes in v2:
time: 125 us; the launch traced here: 124 us
  Pallas kernels  123 us (98%)
  local copies, waits for them, and re-layouts  1.88 us (2%)
    pallas_call x1, Pallas kernels, on_layers(): pl.pallas_call(functools.partial(fused_kernel, levels, spare), out_shape=...  123 us

profile of v2, /device:TPU:0, one launch (start us, length us, event | category | flops | bytes accessed | tf_op | source)
XLA Modules:
  0.0 124.5 jit_solution(4311986392449869724)
XLA Ops:
  0.0 122.6 %layer.1 = bf16[128,2048]{1,0:T(8,128)(2,1)} custom-call(bf16[128,2048]{1,0:T(8,128)(2,1)} %tokens.1, s32[8,128]{1,0:T(8,128)} %bitcast.2, f32[8,128]{1,0:T(8,128)} %bitcast.3, bf16[1,2048,768]{2,1,0:T(8,128)(2,1)} %wg.1, bf16[1,2048,768]{2,1,0:T(8,128)(2,1)} %wu.1, bf16[1,768,2048]{2,1,0:T(8,128)(2,1)} %wd.1), custom_call_target="tpu_custom_call" | custom-call | tf_op jit(solution)/shard_map/layer/pallas_call | solution.py:475
  122.6 1.9 %copy.8 = bf16[128,2048]{1,0:T(8,128)(2,1)} copy(bf16[128,2048]{1,0:T(8,128)(2,1)} %layer.1) | data formatting | bytes 1048576

commit v3 on v2

--- a/solution.py
+++ b/solution.py
@@ -14,44 +14,42 @@
 
 
 ORDER = [
-    ("all", "Start"), ("end", "Sr", 0), ("end", "Lw", 1), ("end", "Ss", 1), ("end", "T"),
-    ("end", "Sd", 0), ("end", "Bs"), ("mid", "Sr", 0), ("mid", "Lr", 2, 0), ("mid", "Lr", 1, 0),
-    ("mid", "Lr", 2, 1), ("mid", "Ss", 2), ("mid", "Lr", 1, 1), ("mid", "Sd", 0), ("mid", "T"),
-    ("mid", "Ss", 1), ("mid", "Bs"), ("mid", "Bi"), ("mid", "Br", 1, 0), ("mid", "Lr", 3, 1),
-    ("mid", "Lr", 3, 0), ("mid", "Sr", 1),
+    ("all", "Start"), ("end", "Sr", 0), ("end", "Lw", 3), ("end", "T"), ("end", "Ss", 3),
+    ("end", "Lw", 1), ("end", "Ss", 1), ("end", "Sd", 0), ("end", "Bs"), ("mid", "Sr", 0),
+    ("mid", "Lr", 1, 0), ("mid", "Lr", 2, 0), ("mid", "T"), ("mid", "Lr", 2, 1), ("mid", "Ss", 2),
+    ("mid", "Lr", 1, 1), ("mid", "Sd", 0), ("mid", "Bi"), ("mid", "Ss", 1), ("mid", "Lr", 3, 0),
     ("all", "C", 0, [
-        ("end", "Sr", 1), ("end", "Lw", 2), ("mid", "Sr", 2), ("mid", "Ss", 3), ("mid", "Br", 2, 1),
-        ("all", "Swap"),
+        ("end", "Sr", 1), ("all", "Swap"),
     ]),
-    ("end", "Ss", 2), ("end", "Bw", 1), ("end", "Sd", 1), ("end", "Sr", 2), ("mid", "Br", 2, 0),
-    ("mid", "Sd", 1), ("mid", "Br", 1, 1),
+    ("end", "Lw", 2), ("end", "Ss", 2), ("end", "Sr", 2), ("end", "Bw", 1), ("end", "Sd", 1),
+    ("end", "Sr", 3), ("mid", "Lr", 3, 1), ("mid", "Sr", 1), ("mid", "Sr", 2), ("mid", "Br", 2, 0),
+    ("mid", "Br", 1, 0), ("mid", "Br", 2, 1), ("mid", "Ss", 3), ("mid", "Sd", 1), ("mid", "Br", 3, 0),
+    ("mid", "Br", 1, 1),
     ("all", "C", 1, [
-        ("mid", "Br", 3, 0), ("mid", "Br", 3, 1),
     ]),
-    ("end", "Lw", 3), ("end", "Ss", 3), ("end", "De", 1, 0), ("end", "De", 1, 1), ("end", "Bw", 2),
-    ("end", "Sr", 3), ("end", "Sd", 2), ("end", "F1", 1), ("mid", "Sr", 3), ("mid", "F1", 1),
-    ("mid", "Sd", 2),
+    ("end", "De", 1, 1), ("end", "Bw", 2), ("end", "Sd", 2), ("end", "De", 1, 0), ("end", "F1", 1),
+    ("mid", "Sd", 2), ("mid", "Br", 3, 1), ("mid", "Sr", 3), ("mid", "F1", 1),
     ("all", "C", 2, [
-        ("mid", "F2", 1), ("mid", "Sd", 3),
+        ("end", "Sd", 3),
     ]),
-    ("end", "Sd", 3), ("end", "De", 2, 0), ("end", "De", 2, 1), ("end", "Bw", 3), ("mid", "F1", 2),
+    ("end", "F1", 2), ("end", "De", 2, 0), ("end", "De", 2, 1), ("end", "F2", 1), ("end", "Bw", 3),
+    ("mid", "Bs"), ("mid", "Sd", 3),
     ("all", "C", 3, [
-        ("end", "F2", 1), ("mid", "Dm", 2, 0),
+        ("mid", "Dm", 2, 1), ("mid", "F1", 2), ("mid", "Dm", 2, 0), ("mid", "F2", 1),
     ]),
-    ("end", "De", 3, 0), ("end", "F1", 3), ("end", "De", 3, 1), ("end", "F2", 3), ("end", "F1", 2),
-    ("end", "F3", 3, 0), ("end", "Ce", 3, 0), ("end", "F3", 1, 0), ("end", "F3", 1, 1),
-    ("end", "F3", 3, 1), ("end", "Ce", 3, 1), ("end", "F2", 2), ("end", "F1", 0), ("end", "Ce", 1, 0),
-    ("end", "Dw", 0), ("end", "F3", 2, 0), ("end", "Ce", 2, 0), ("end", "F3", 2, 1),
-    ("end", "Ce", 2, 1), ("end", "Dw", 1), ("end", "F1", 4), ("end", "Ce", 1, 1), ("end", "F2", 0),
-    ("end", "Cw", 1), ("end", "F2", 4), ("end", "F3", 0, 0), ("end", "Cw", 0), ("end", "F3", 0, 1),
-    ("end", "F3", 4, 0), ("end", "F3", 4, 1), ("mid", "F1", 3), ("mid", "Dm", 2, 1),
-    ("mid", "Dm", 3, 0), ("mid", "F3", 1, 0), ("mid", "Dw", 0), ("mid", "F2", 3), ("mid", "Dm", 3, 1),
-    ("mid", "Dw", 1), ("mid", "F1", 4), ("mid", "Dm", 1, 0), ("mid", "F3", 1, 1), ("mid", "F2", 2),
-    ("mid", "F3", 3, 1), ("mid", "F3", 3, 0), ("mid", "Dm", 1, 1), ("mid", "Cm", 3, 1),
-    ("mid", "F1", 0), ("mid", "Cm", 3, 0), ("mid", "F2", 4), ("mid", "F3", 2, 0), ("mid", "F2", 0),
-    ("mid", "Cm", 1, 1), ("mid", "Cm", 2, 0), ("mid", "Cm", 1, 0), ("mid", "F3", 2, 1),
-    ("mid", "Cm", 2, 1), ("mid", "F3", 4, 0), ("mid", "F3", 4, 1), ("mid", "F3", 0, 1),
-    ("mid", "Cw", 0), ("mid", "F3", 0, 0), ("mid", "Cw", 1),
+    ("end", "De", 3, 0), ("end", "F2", 2), ("end", "F1", 3), ("end", "De", 3, 1), ("end", "F3", 2, 0),
+    ("end", "Ce", 2, 0), ("end", "F3", 2, 1), ("end", "Ce", 2, 1), ("end", "F2", 3), ("end", "F1", 0),
+    ("end", "F3", 1, 0), ("end", "Ce", 1, 0), ("end", "F3", 1, 1), ("end", "F3", 3, 1),
+    ("end", "Dw", 0), ("end", "Ce", 1, 1), ("end", "F3", 3, 0), ("end", "Ce", 3, 1), ("end", "Dw", 1),
+    ("end", "F1", 4), ("end", "F2", 0), ("end", "Ce", 3, 0), ("end", "F2", 4), ("end", "Cw", 1),
+    ("end", "F3", 4, 1), ("end", "Cw", 0), ("end", "F3", 4, 0), ("end", "F3", 0, 0),
+    ("end", "F3", 0, 1), ("mid", "F1", 3), ("mid", "Dm", 3, 0), ("mid", "Dm", 3, 1),
+    ("mid", "Dm", 1, 0), ("mid", "F3", 1, 1), ("mid", "F2", 3), ("mid", "F2", 2), ("mid", "F3", 3, 0),
+    ("mid", "Cm", 3, 0), ("mid", "F3", 3, 1), ("mid", "Dw", 1), ("mid", "Dm", 1, 1), ("mid", "Dw", 0),
+    ("mid", "F1", 0), ("mid", "Cm", 3, 1), ("mid", "F3", 2, 1), ("mid", "F3", 1, 0), ("mid", "F1", 4),
+    ("mid", "F3", 2, 0), ("mid", "Cm", 1, 0), ("mid", "F2", 0), ("mid", "Cm", 2, 0),
+    ("mid", "Cm", 2, 1), ("mid", "Cm", 1, 1), ("mid", "F2", 4), ("mid", "Cw", 1), ("mid", "F3", 0, 0),
+    ("mid", "F3", 0, 1), ("mid", "F3", 4, 1), ("mid", "F3", 4, 0), ("mid", "Cw", 0),
 ]
 
 
@@ -79,8 +77,8 @@
     columns = chips // levels
     cap = xs.shape[1] // columns
     main = rows - spare
-    cut = (main // 2 + 15) // 16 * 16
-    bcut = spare // 2
+    cut = (main // 2 + 7) // 8 * 8
+    bcut = (spare // 2 + 7) // 8 * 8
     whole = (pl.ds(0, rows // 2), pl.ds(rows // 2, rows // 2))
     part_rows = (pl.ds(0, cut), pl.ds(cut, main - cut))
     tail_rows = (pl.ds(main, bcut), pl.ds(main + bcut, spare - bcut))
@@ -90,9 +88,9 @@
     inner = (side, mid * flip(level, 3) + (1 - mid) * flip(level, 1))
     lev = [
         level,
-        flip(level, 1),
-        mid * flip(level, 3) + (1 - mid) * flip(level, 2),
-        mid * flip(level, 2) + (1 - mid) * flip(level, 3),
+        mid * flip(level, 1) + (1 - mid) * flip(level, 2),
+        flip(level, 3),
+        mid * flip(level, 2) + (1 - mid) * flip(level, 1),
     ]
     me = col * levels + level
     others = [(flip(col, m // levels), flip(level, m % levels)) for m in range(1, chips)]
@@ -166,16 +164,20 @@
         for i in range(2, 6):
             spread[k][i].wait_recv()
 
+    there = 1 + 2 * mid
     def line_copies(view, own, s, r):
         out = []
         for i in range(2):
             out.append(
                 [
-                    link(own(i), view(1, i), s.at[0, i], r.at[1, i], mate),
+                    link(own(i), view(there, i), s.at[0, i], r.at[there, i], mate),
                     link(own(i), view(2, i), s.at[1, i], r.at[2, i], inner),
                     link(view(1, i), view(3, i), s.at[2, i], r.at[3, i], inner),
-                    link(view(2, i), view(2, i), s.at[3, i], r.at[2, i], mate),
-                    link(view(3, i), view(3, i), s.at[4, i], r.at[3, i], mate),
+                    link(view(2, i), view(1, i), s.at[3, i], r.at[1, i], mate),
+                    link(view(3, i), view(2, i), s.at[4, i], r.at[2, i], mate),
+                    link(view(1, i), view(1, i), s.at[0, i], r.at[1, i], mate),
+                    link(view(2, i), view(2, i), s.at[0, i], r.at[2, i], mate),
+                    link(view(3, i), view(3, i), s.at[0, i], r.at[3, i], mate),
                 ]
             )
         return out
@@ -200,10 +202,10 @@
 
     def line_wait(copies, k):
         for i in range(2):
-            copies[i][k - 1].wait_recv()
+            copies[i][k + 4].wait_recv()
 
     def line_relay(copies, k, i):
-        copies[i][k - 1].wait_recv()
+        copies[i][k + 4].wait_recv()
         copies[i][k + 1].start()
 
     small = [
@@ -319,7 +321,7 @@
     def chain(view, land, s, r):
         send_end, send_mid = {}, {}
         for i in range(2):
-            for k, end_slot, mid_slot in ((3, 3, 4), (2, 2, 1), (1, 0, 0)):
+            for k, end_slot, mid_slot in ((3, 0, 4), (2, 3, 1), (1, 2, 0)):
                 send_end[k, i] = link(view(k, i), land(end_slot, i), s.at[k, i], r.at[end_slot, i], mate)
                 send_mid[k, i] = link(
                     view(k, i), land(mid_slot, i), s.at[k, i], r.at[mid_slot, i], mate if k == 1 else inner
@@ -440,23 +442,15 @@
             copies[i][0].wait_send()
         for c in (rows_chain, tail_chain):
             c[0][1, i].wait_send()
+            c[0][2, i].wait_send()
+            c[0][3, i].wait_send()
 
     @pl.when(mid == 1)
     def _():
         for i in range(2):
             for copies in (lines, bands):
-                for copy in copies[i][1:]:
+                for copy in copies[i][1:5]:
                     copy.wait_send()
-            for c in (rows_chain, tail_chain):
-                c[1][2, i].wait_send()
-                c[1][3, i].wait_send()
-
-    @pl.when(mid == 0)
-    def _():
-        for i in range(2):
-            for c in (rows_chain, tail_chain):
-                c[0][2, i].wait_send()
-                c[0][3, i].wait_send()
 
 
 def on_layers(levels, tokens, expert_ids, route_weights, w_gate, w_up, w_down):
@@ -468,7 +462,7 @@
     columns = chips // levels
     spare = tok_rows // 4
     main = tok_rows - spare
-    cut = (main // 2 + 15) // 16 * 16
+    cut = (main // 2 + 7) // 8 * 8
     anywhere = pl.BlockSpec(memory_space=pl.ANY)
     vmem = pltpu.VMEM
     dma = pltpu.SemaphoreType.DMA

time: 125 us -> 124 us (level)
  no operation moved by 1% of the time
where the time goes in v3:
time: 124 us
  Pallas kernels  122 us (98%)
  local copies, waits for them, and re-layouts  1.88 us (2%)
    pallas_call x1, Pallas kernels, on_layers(): pl.pallas_call(functools.partial(fused_kernel, levels, spare), out_shape=...  122 us

profile of v3, /device:TPU:0, one launch (start us, length us, event | category | flops | bytes accessed | tf_op | source)
XLA Modules:
  0.0 123.6 jit_solution(14743581837767182053)
XLA Ops:
  0.0 121.7 %layer.1 = bf16[128,2048]{1,0:T(8,128)(2,1)} custom-call(bf16[128,2048]{1,0:T(8,128)(2,1)} %tokens.1, s32[8,128]{1,0:T(8,128)} %bitcast.2, f32[8,128]{1,0:T(8,128)} %bitcast.3, bf16[1,2048,768]{2,1,0:T(8,128)(2,1)} %wg.1, bf16[1,2048,768]{2,1,0:T(8,128)(2,1)} %wu.1, bf16[1,768,2048]{2,1,0:T(8,128)(2,1)} %wd.1), custom_call_target="tpu_custom_call" | custom-call | tf_op jit(solution)/shard_map/layer/pallas_call | solution.py:469
  121.7 1.9 %copy.8 = bf16[128,2048]{1,0:T(8,128)(2,1)} copy(bf16[128,2048]{1,0:T(8,128)(2,1)} %layer.1) | data formatting | bytes 1048576

commit v4 on v3

--- a/solution.py
+++ b/solution.py
@@ -66,7 +66,7 @@
 def fused_kernel(
     levels, spare, tokens, ids, gains, wg, wu, wd, out, ids_v, gains_v, mine, shares, slots, wgs, wus, wds, every,
     part, xs, ys, backs, first, second, row_in, plane_in, gs, gr, zs, zr, bs, br, ps, pr, cs, cr, ds, dr, ss, sr, ws,
-    wr, local
+    wr, known, local
 ):
     side, level = lax.axis_index("side"), lax.axis_index("lane")
     col, core = side // 2, side % 2
@@ -95,46 +95,66 @@
     me = col * levels + level
     others = [(flip(col, m // levels), flip(level, m % levels)) for m in range(1, chips)]
 
+    def on_mid(do):
+        pl.when(mid == 1)(do)
+
+    def on_end(do):
+        pl.when(mid == 0)(do)
+
+    def tell(sem, device):
+        pl.semaphore_signal(sem, inc=1, device_id=device, device_id_type=MESH)
+
+    barrier = pltpu.get_barrier_semaphore()
+    for device in (dev_x, dev_y, mate, twin):
+        tell(barrier, device)
+    on_mid(lambda: tell(barrier, inner))
     fetch = [pltpu.make_async_copy(ids, ids_v, local.at[0]), pltpu.make_async_copy(gains, gains_v, local.at[1])]
-    for copy in fetch:
-        copy.start()
-    barrier = pltpu.get_barrier_semaphore()
-    friends = [(q * 2 + core, z) for q, z in others] + [twin]
-    for device in friends:
-        pl.semaphore_signal(barrier, inc=1, device_id=device, device_id_type=MESH)
     keep = [
         pltpu.make_async_copy(tokens, every.at[0, 0], local.at[2]),
         pltpu.make_async_copy(wg.at[0], wgs.at[0], local.at[3]),
         pltpu.make_async_copy(wu.at[0], wus.at[0], local.at[4]),
         pltpu.make_async_copy(wd.at[0], wds.at[0], local.at[5]),
     ]
-    for copy in keep:
+    for copy in fetch + keep:
         copy.start()
-    for copy in fetch:
-        copy.wait()
-    number = lax.broadcasted_iota(jnp.int32, (2 * chips, rows), 0)
-    table = jnp.zeros((2 * chips, rows), F32)
-    for k in range(ids_v.shape[0]):
-        table = table + jnp.where(ids_v[k : k + 1] == number, gains_v[k : k + 1], 0.0)
-    for q in range(columns):
-        for z in range(levels):
-            for c in range(2):
-                e = (q * 2 + c) * levels + z
-                mine[q * levels + z, c : c + 1, :] = table[e : e + 1, :]
-            mine[q * levels + z, 2:8, :] = jnp.zeros((6, rows), F32)
-    shares[me] = mine[me]
-    pl.semaphore_wait(barrier, len(friends))
+    pl.semaphore_wait(barrier, 4 + mid)
+
+    def make_mine():
+        for copy in fetch:
+            copy.wait()
+        number = lax.broadcasted_iota(jnp.int32, (2 * chips, rows), 0)
+        table = jnp.zeros((2 * chips, rows), F32)
+        for k in range(ids_v.shape[0]):
+            table = table + jnp.where(ids_v[k : k + 1] == number, gains_v[k : k + 1], 0.0)
+        for q in range(columns):
+            for z in range(levels):
+                for c in range(2):
+                    e = (q * 2 + c) * levels + z
+                    mine[q * levels + z, c : c + 1, :] = table[e : e + 1, :]
+                mine[q * levels + z, 2:8, :] = jnp.zeros((6, rows), F32)
+        shares[me] = mine[me]
+
+    def hear_all():
+        for device in (dev_x, dev_y):
+            tell(known.at[0], device)
+        pl.semaphore_wait(known.at[0], 2)
+        tell(known.at[1], mate)
+        on_mid(lambda: tell(known.at[1], inner))
+        pl.semaphore_wait(known.at[1], 1 + mid)
+
+        @pl.when(mid == 1)
+        def _():
+            tell(known.at[2], mate)
+            tell(known.at[2], inner)
+
+        pl.semaphore_wait(known.at[2], 1)
+        on_mid(lambda: tell(known.at[3], mate))
+        on_end(lambda: pl.semaphore_wait(known.at[3], 1))
 
     def link(src, dst, s, r, device):
         return pltpu.make_async_remote_copy(
             src_ref=src, dst_ref=dst, send_sem=s, recv_sem=r, device_id=device, device_id_type=MESH
         )
-
-    def on_mid(do):
-        pl.when(mid == 1)(do)
-
-    def on_end(do):
-        pl.when(mid == 0)(do)
 
     def spread_copies(k):
         p, q = whole if k == 0 else part_rows
@@ -373,11 +393,13 @@
         spread[0][1].start()
         line_send(lines)
         on_mid(lambda: line_send_inner(lines))
-        for copy in small:
-            copy.start()
         spread[0][2].start()
         spread[0][3].start()
         for copy in swap:
+            copy.start()
+        make_mine()
+        hear_all()
+        for copy in small:
             copy.start()
 
     def make_tables():
@@ -505,6 +527,7 @@
             dma((chips - 1,)),
             dma((3,)),
             dma((3,)),
+            pltpu.SemaphoreType.REGULAR((4,)),
             dma((6,)),
         ],
         compiler_params=pltpu.CompilerParams(

time: 124 us -> 121 us (0.976)
  Pallas kernels: 122 us -> 119 us
    pallas_call x1, Pallas kernels: 122 us -> 119 us  [on_layers(): pl.pallas_call(functools.partial(fused_kernel, levels, spare), out_shape=...]
where the time goes in v4:
time: 121 us
  Pallas kernels  119 us (98%)
  local copies, waits for them, and re-layouts  1.88 us (2%)
    pallas_call x1, Pallas kernels, on_layers(): pl.pallas_call(functools.partial(fused_kernel, levels, spare), out_shape=...  119 us

profile of v4, /device:TPU:0, one launch (start us, length us, event | category | flops | bytes accessed | tf_op | source)
XLA Modules:
  0.0 120.6 jit_solution(399380455239267917)
XLA Ops:
  0.0 118.7 %layer.1 = bf16[128,2048]{1,0:T(8,128)(2,1)} custom-call(bf16[128,2048]{1,0:T(8,128)(2,1)} %tokens.1, s32[8,128]{1,0:T(8,128)} %bitcast.2, f32[8,128]{1,0:T(8,128)} %bitcast.3, bf16[1,2048,768]{2,1,0:T(8,128)(2,1)} %wg.1, bf16[1,2048,768]{2,1,0:T(8,128)(2,1)} %wu.1, bf16[1,768,2048]{2,1,0:T(8,128)(2,1)} %wd.1), custom_call_target="tpu_custom_call" | custom-call | tf_op jit(solution)/shard_map/layer/pallas_call | solution.py:491
  118.7 1.9 %copy.8 = bf16[128,2048]{1,0:T(8,128)(2,1)} copy(bf16[128,2048]{1,0:T(8,128)(2,1)} %layer.1) | data formatting | bytes 1048576

commit v5 on v4

--- a/solution.py
+++ b/solution.py
@@ -531,7 +531,7 @@
             dma((6,)),
         ],
         compiler_params=pltpu.CompilerParams(
-            collective_id=0, has_side_effects=True, vmem_limit_bytes=62 * 2**20
+            collective_id=0, has_side_effects=True, vmem_limit_bytes=53 * 2**20
         ),
         name="layer",
     )(tokens, expert_ids.T, route_weights.T, w_gate, w_up, w_down)

time: 121 us -> 120 us (level)
  no operation moved by 1% of the time
where the time goes in v5:
time: 120 us
  Pallas kernels  118 us (98%)
  local copies, waits for them, and re-layouts  2.17 us (2%)
    pallas_call x1, Pallas kernels, on_layers(): pl.pallas_call(functools.partial(fused_kernel, levels, spare), out_shape=...  118 us

profile of v5, /device:TPU:0, one launch (start us, length us, event | category | flops | bytes accessed | tf_op | source)
XLA Modules:
  0.0 120.1 jit_solution(4082389883779789501)
XLA Ops:
  0.0 0.0 copy-start
  0.0 0.7 copy-done
  0.7 0.0 copy-start.1
  0.7 0.7 copy-done.1
  1.4 117.9 %layer.1 = bf16[128,2048]{1,0:T(8,128)(2,1)S(1)} custom-call(bf16[128,2048]{1,0:T(8,128)(2,1)} %tokens.1, s32[8,128]{1,0:T(8,128)S(1)} %bitcast.2, f32[8,128]{1,0:T(8,128)S(1)} %bitcast.3, bf16[1,2048,768]{2,1,0:T(8,128)(2,1)} %wg.1, bf16[1,2048,768]{2,1,0:T(8,128)(2,1)} %wu.1, bf16[1,768,2048]{2,1,0:T(8,128)(2,1)} %wd.1), custom_call_target="tpu_custom_call" | custom-call | tf_op jit(solution)/shard_map/layer/pallas_call | solution.py:491
  119.3 0.8 copy.8
Async XLA Ops:
  0.0 0.7 copy-start
  0.7 0.7 copy-start.1

commit v6 on v5

--- a/solution.py
+++ b/solution.py
@@ -486,6 +486,7 @@
     main = tok_rows - spare
     cut = (main // 2 + 7) // 8 * 8
     anywhere = pl.BlockSpec(memory_space=pl.ANY)
+    stay = functools.partial(pltpu.with_memory_space_constraint, memory_space=pltpu.HBM)
     vmem = pltpu.VMEM
     dma = pltpu.SemaphoreType.DMA
     return pl.pallas_call(
@@ -534,7 +535,7 @@
             collective_id=0, has_side_effects=True, vmem_limit_bytes=53 * 2**20
         ),
         name="layer",
-    )(tokens, expert_ids.T, route_weights.T, w_gate, w_up, w_down)
+    )(tokens, stay(expert_ids.T), stay(route_weights.T), w_gate, w_up, w_down)
 
 
 def expert_ffn(rows, gate_proj, up_proj, down_proj):

time: 120 us -> 119 us (level)
  local copies, waits for them, and re-layouts: 2.17 us -> 0.8 us
    unnamed x5 -> x1, local copies, waits for them, and re-layouts: 2.17 us -> 0.8 us
where the time goes in v6:
time: 119 us
  Pallas kernels  118 us (99%)
    pallas_call x1, Pallas kernels, on_layers(): pl.pallas_call(functools.partial(fused_kernel, levels, spare), out_shape=...  118 us

profile of v6, /device:TPU:0, one launch (start us, length us, event | category | flops | bytes accessed | tf_op | source)
XLA Modules:
  0.0 118.7 jit_solution(6149170930292690975)
XLA Ops:
  0.0 117.9 %layer.1 = bf16[128,2048]{1,0:T(8,128)(2,1)S(1)} custom-call(bf16[128,2048]{1,0:T(8,128)(2,1)} %tokens.1, s32[8,128]{1,0:T(8,128)} %bitcast.2, f32[8,128]{1,0:T(8,128)} %bitcast.3, bf16[1,2048,768]{2,1,0:T(8,128)(2,1)} %wg.1, bf16[1,2048,768]{2,1,0:T(8,128)(2,1)} %wu.1, bf16[1,768,2048]{2,1,0:T(8,128)(2,1)} %wd.1), custom_call_target="tpu_custom_call" | custom-call | tf_op jit(solution)/shard_map/layer/pallas_call | solution.py:492
  117.9 0.8 copy.8
